TPU v7x, 32 devices: a whole 2x2x4 slice. The times are simulated.
32 devices in a mesh: gz: 8 (over z, x), gy: 4 (over y, core).
Axes of the slice: x: 2, y: 2, z: 4, core: 2. Of those that a mesh axis runs over, the one named last changes fastest.
Arguments:
- source: float32 [32, 64, 512], P('gz', 'gy'), may hold values from -8 to 8
- conduct: float32 [32, 64, 512], P('gz', 'gy'), may hold values from 0.5 to 4
Outputs:
- adjoint: float32 [32, 64, 512], P('gz', 'gy')
- residual: float32 [32, 64, 512], P('gz', 'gy')
All inputs are finite; a program needn't handle non-finite values.
Results may differ from a plain program's by a relative error of at most 0.0003.
Values sent between devices are 32-bit elements; how exact they have to be, the bound alone decides.
A program may use at most 64 MiB of HBM per device.

v0:
```python
import jax
import jax.numpy as jnp
from jax import lax
from jax.sharding import PartitionSpec as P

DEGREE = 3
COARSE_DEGREE = 4
CYCLES = 2


cheb_low = 0.3
cheb_high = 1.9
heat_step = 4.0


def padded_2(shard, sides, width):
    for axis, dim in sides:
        devices, length = (lax.axis_size(axis), shard.shape[dim])
        up = [(i, (i + 1) % devices) for i in range(devices)]
        down = [(j, i) for i, j in up]
        last = lax.slice_in_dim(shard, length - width, length, axis=dim)
        first = lax.slice_in_dim(shard, 0, width, axis=dim)
        before = lax.ppermute(last, axis, up)
        after = lax.ppermute(first, axis, down)
        shard = jnp.concatenate([before, shard, after], axis=dim)
    return shard


def spread_apply(field, conduct, scale):
    w = conduct * field
    padded = padded_2(w, (("gz", 0), ("gy", 1)), 1)
    beside = padded[2:, 1:-1, :] + padded[:-2, 1:-1, :]
    beside = beside + padded[1:-1, 2:, :] + padded[1:-1, :-2, :]
    wide = jnp.pad(w, ((0, 0), (0, 0), (1, 1)))
    beside = beside + wide[:, :, 2:] + wide[:, :, :-2]
    return field + scale * (6.0 * w - beside)


def deep_halo(field):
    return padded_2(field, (("gz", 0), ("gy", 1)), DEGREE)


def trim(field):
    return field[1:-1, 1:-1, :]


def margin_apply(field, conduct, scale):
    w = conduct * field
    beside = w[2:, 1:-1, :] + w[:-2, 1:-1, :]
    beside = beside + w[1:-1, 2:, :] + w[1:-1, :-2, :]
    inner = trim(w)
    wide = jnp.pad(inner, ((0, 0), (0, 0), (1, 1)))
    beside = beside + wide[:, :, 2:] + wide[:, :, :-2]
    return trim(field) + scale * (6.0 * inner - beside)


def margin_smooth(rhs_pad, cond_pad, start_pad, scale, steps):
    theta = (cheb_high + cheb_low) / 2.0
    delta = (cheb_high - cheb_low) / 2.0
    sigma = theta / delta
    rho = 1.0 / sigma
    field = jnp.zeros_like(rhs_pad) if start_pad is None else start_pad
    rhs = rhs_pad
    cond = cond_pad
    inverse = 1.0 / (1.0 + 6.0 * scale * cond_pad)
    change = None
    for step in range(steps):
        image = margin_apply(field, cond, scale)
        rhs = trim(rhs)
        inverse = trim(inverse)
        cond = trim(cond)
        field = trim(field)
        correct = inverse * (rhs - image)
        if step == 0:
            change = correct / theta
        else:
            rho_next = 1.0 / (2.0 * sigma - rho)
            change = rho_next * rho * trim(change) + 2.0 * rho_next / delta * correct
            rho = rho_next
        field = field + change
    return field


def restrict(field):
    z, y, x = field.shape
    return field.reshape(z // 2, 2, y // 2, 2, x // 2, 2).mean(axis=(1, 3, 5))


def prolong(field):
    return jnp.repeat(jnp.repeat(jnp.repeat(field, 2, 0), 2, 1), 2, 2)


def smooth(apply_fn, rhs, start, inv_diag, steps):
    theta = (cheb_high + cheb_low) / 2.0
    delta = (cheb_high - cheb_low) / 2.0
    sigma = theta / delta
    rho = 1.0 / sigma
    if start is None:
        correct = inv_diag * rhs
        change = correct / theta
        field = change
    else:
        correct = inv_diag * (rhs - apply_fn(start))
        change = correct / theta
        field = start + change
    for step in range(steps - 1):
        rho_next = 1.0 / (2.0 * sigma - rho)
        correct = inv_diag * (rhs - apply_fn(field))
        change = rho_next * rho * change + 2.0 * rho_next / delta * correct
        field = field + change
        rho = rho_next
    return field


def bind(apply_fn, conduct, scale):

    def inner(field):
        return apply_fn(field, conduct, scale)

    return inner


def coarse_solve(rhs_low, low_cond, scale):
    diag = 1.0 / (1.0 + 6.0 * scale * low_cond)
    return smooth(bind(spread_apply, low_cond, scale), rhs_low, None, diag, COARSE_DEGREE)


def vcycle(rhs, conducts, scales, cond_pad):
    ops = [bind(spread_apply, conducts[i], scales[i]) for i in range(2)]
    diags = [1.0 / (1.0 + 6.0 * scales[i] * conducts[i]) for i in range(2)]
    rhs_pad = None
    rhs_pad = deep_halo(rhs)
    fine = margin_smooth(rhs_pad, cond_pad, None, scales[0], DEGREE)
    rhs_mid = restrict(rhs - ops[0](fine))
    middle = smooth(ops[1], rhs_mid, None, diags[1], DEGREE)
    rhs_low = restrict(rhs_mid - ops[1](middle))
    lowest = coarse_solve(rhs_low, conducts[2], scales[2])
    middle = smooth(ops[1], rhs_mid, middle + prolong(lowest), diags[1], DEGREE)
    start_pad = deep_halo(fine + prolong(middle))
    fine = margin_smooth(rhs_pad, cond_pad, start_pad, scales[0], DEGREE)
    return fine


def local(source, conduct):
    mid_cond = restrict(conduct)
    conducts = [conduct, mid_cond, restrict(mid_cond)]
    scales = [heat_step, heat_step / 4.0, heat_step / 16.0]
    cond_pad = None
    cond_pad = deep_halo(conduct)
    adjoint = jnp.zeros_like(source)
    remain = source
    for cycle in range(CYCLES):
        adjoint = adjoint + vcycle(remain, conducts, scales, cond_pad)
        remain = source - spread_apply(adjoint, conduct, heat_step)
    return (adjoint, remain)


def solution(mesh):
    placed = (P("gz", "gy", None), P("gz", "gy", None))
    return jax.shard_map(
        local,
        mesh=mesh,
        in_specs=placed,
        out_specs=(P("gz", "gy", None), P("gz", "gy", None)),
        check_vma=False,
    )
```

profile of v0, /device:TPU:0, one launch (start us, length us, event | category | flops | bytes accessed | tf_op | source)
XLA Modules:
  0.0 333.4 jit_solution(4471759033925861064)
XLA Ops:
  1.7 3.0 collective-permute-start
  5.7 3.1 collective-permute-start.5
  8.8 4.7 %collective-permute-start.1 = (f32[3,16,512]{2,1,0:T(8,128)S(1)}, f32[3,16,512]{2,1,0:T(8,128)S(1)}, u32[]{:S(2)}, u32[]{:S(2)}) collective-permute-start(f32[3,16,512]{2,1,0:T(8,128)S(1)} %get-tuple-element.98), channel_id=1, source_target_pairs={{4,0},{8,4},{12,8},{16,12},{20,16},{24,20},{28,24},{0,28},{5,1},{9... | collective-permute-start | bytes 294920 | tf_op jit(solution)/shard_map/ppermute | solution.py:24
  14.5 1.9 collective-permute-done.1
  16.4 1.7 collective-permute-start.3
  21.2 1.9 collective-permute-done.6
  24.5 4.7 %collective-permute-start.8 = (f32[1,16,512]{2,1,0:T(8,128)S(1)}, f32[1,16,512]{2,1,0:T(8,128)S(1)}, u32[]{:S(2)}, u32[]{:S(2)}) collective-permute-start(f32[1,16,512]{2,1,0:T(8,128)S(1)} %get-tuple-element.95), channel_id=1, source_target_pairs={{4,0},{8,4},{12,8},{16,12},{20,16},{24,20},{28,24},{0,28},{5,1},{9... | collective-permute-start | bytes 98312 | tf_op jit(solution)/shard_map/ppermute | solution.py:24
  29.2 1.9 collective-permute-done.9
  32.5 9.7 %reshape.193 = f32[2,2,8,2,256,2]{5,4,3,2,1,0:T(8,128)} reshape(f32[4,16,512]{2,1,0:T(8,128)S(1)} %copy-done) | data formatting | bytes 262144 | tf_op jit(solution)/shard_map/reshape | solution.py:86
  42.3 4.0 %reduce_sum.60 = f32[2,8,256]{2,1,0:T(8,128)S(1)} reduce(f32[2,2,8,2,256,2]{5,4,3,2,1,0:T(8,128)} %reshape.193, f32[]{:T(128)} %constant.27.clone.1), dimensions={1,3,5}, to_apply=%region_0.0 | reduce | flops 28672 | bytes 147460 | tf_op jit(solution)/shard_map/reduce_sum | solution.py:86
  46.5 9.8 %reshape.194 = f32[2,2,8,2,256,2]{5,4,3,2,1,0:T(8,128)} reshape(f32[4,16,512]{2,1,0:T(8,128)S(1)} %fusion.71) | data formatting | bytes 262144 | tf_op jit(solution)/shard_map/reshape | solution.py:86
  56.2 4.0 %reduce_sum.61 = f32[2,8,256]{2,1,0:T(8,128)S(1)} reduce(f32[2,2,8,2,256,2]{5,4,3,2,1,0:T(8,128)} %reshape.194, f32[]{:T(128)} %constant.27.clone.1), dimensions={1,3,5}, to_apply=%region_1.0 | reduce | flops 28672 | bytes 147460 | tf_op jit(solution)/shard_map/reduce_sum | solution.py:86
  60.3 4.7 %collective-permute-start.12 = (f32[1,8,256]{2,1,0:T(8,128)S(1)}, f32[1,8,256]{2,1,0:T(8,128)S(1)}, u32[]{:S(2)}, u32[]{:S(2)}) collective-permute-start(f32[1,8,256]{2,1,0:T(8,128)S(1)} %get-tuple-element.149), channel_id=1, source_target_pairs={{4,0},{8,4},{12,8},{16,12},{20,16},{24,20},{28,24},{0,28},{5,1},{9... | collective-permute-start | bytes 24584 | tf_op jit(solution)/shard_map/ppermute | solution.py:24
  70.7 4.7 %collective-permute-start.16 = (f32[1,8,256]{2,1,0:T(8,128)S(1)}, f32[1,8,256]{2,1,0:T(8,128)S(1)}, u32[]{:S(2)}, u32[]{:S(2)}) collective-permute-start(f32[1,8,256]{2,1,0:T(8,128)S(1)} %get-tuple-element.147), channel_id=1, source_target_pairs={{4,0},{8,4},{12,8},{16,12},{20,16},{24,20},{28,24},{0,28},{5,1},{9... | collective-permute-start | bytes 24584 | tf_op jit(solution)/shard_map/ppermute | solution.py:24
  78.4 1.8 collective-permute-done.19
  80.4 4.8 %collective-permute-start.20 = (f32[1,8,256]{2,1,0:T(8,128)S(1)}, f32[1,8,256]{2,1,0:T(8,128)S(1)}, u32[]{:S(2)}, u32[]{:S(2)}) collective-permute-start(f32[1,8,256]{2,1,0:T(8,128)S(1)} %get-tuple-element.143), channel_id=1, source_target_pairs={{4,0},{8,4},{12,8},{16,12},{20,16},{24,20},{28,24},{0,28},{5,1},{9... | collective-permute-start | bytes 24584 | tf_op jit(solution)/shard_map/ppermute | solution.py:24
  88.1 1.8 collective-permute-done.23
  90.7 4.8 %collective-permute-start.24 = (f32[1,4,128]{2,1,0:T(4,128)S(1)}, f32[1,4,128]{2,1,0:T(4,128)S(1)}, u32[]{:S(2)}, u32[]{:S(2)}) collective-permute-start(f32[1,4,128]{2,1,0:T(4,128)S(1)} %bitcast_multiply_fusion.6), channel_id=1, source_target_pairs={{4,0},{8,4},{12,8},{16,12},{20,16},{24,20},{28,24},{0,28},{5,1},{9... | collective-permute-start | bytes 6152 | tf_op jit(solution)/shard_map/ppermute | solution.py:24
  98.3 1.8 collective-permute-done.27
  100.2 4.8 %collective-permute-start.28 = (f32[1,4,128]{2,1,0:T(4,128)S(1)}, f32[1,4,128]{2,1,0:T(4,128)S(1)}, u32[]{:S(2)}, u32[]{:S(2)}) collective-permute-start(f32[1,4,128]{2,1,0:T(4,128)S(1)} %get-tuple-element.45), channel_id=1, source_target_pairs={{4,0},{8,4},{12,8},{16,12},{20,16},{24,20},{28,24},{0,28},{5,1},{9... | collective-permute-start | bytes 6152 | tf_op jit(solution)/shard_map/ppermute | solution.py:24
  107.9 1.8 collective-permute-done.31
  109.7 4.8 %collective-permute-start.32 = (f32[1,4,128]{2,1,0:T(4,128)S(1)}, f32[1,4,128]{2,1,0:T(4,128)S(1)}, u32[]{:S(2)}, u32[]{:S(2)}) collective-permute-start(f32[1,4,128]{2,1,0:T(4,128)S(1)} %get-tuple-element.43), channel_id=1, source_target_pairs={{4,0},{8,4},{12,8},{16,12},{20,16},{24,20},{28,24},{0,28},{5,1},{9... | collective-permute-start | bytes 6152 | tf_op jit(solution)/shard_map/ppermute | solution.py:24
  117.4 1.8 collective-permute-done.35
  119.5 4.8 %collective-permute-start.36 = (f32[1,8,256]{2,1,0:T(8,128)S(1)}, f32[1,8,256]{2,1,0:T(8,128)S(1)}, u32[]{:S(2)}, u32[]{:S(2)}) collective-permute-start(f32[1,8,256]{2,1,0:T(8,128)S(1)} %get-tuple-element.141), channel_id=1, source_target_pairs={{4,0},{8,4},{12,8},{16,12},{20,16},{24,20},{28,24},{0,28},{5,1},{9... | collective-permute-start | bytes 24584 | tf_op jit(solution)/shard_map/ppermute | solution.py:24
  127.2 1.8 collective-permute-done.39
  129.2 4.8 %collective-permute-start.40 = (f32[1,8,256]{2,1,0:T(8,128)S(1)}, f32[1,8,256]{2,1,0:T(8,128)S(1)}, u32[]{:S(2)}, u32[]{:S(2)}) collective-permute-start(f32[1,8,256]{2,1,0:T(8,128)S(1)} %get-tuple-element.139), channel_id=1, source_target_pairs={{4,0},{8,4},{12,8},{16,12},{20,16},{24,20},{28,24},{0,28},{5,1},{9... | collective-permute-start | bytes 24584 | tf_op jit(solution)/shard_map/ppermute | solution.py:24
  137.0 1.8 collective-permute-done.43
  138.9 4.8 %collective-permute-start.44 = (f32[1,8,256]{2,1,0:T(8,128)S(1)}, f32[1,8,256]{2,1,0:T(8,128)S(1)}, u32[]{:S(2)}, u32[]{:S(2)}) collective-permute-start(f32[1,8,256]{2,1,0:T(8,128)S(1)} %get-tuple-element.137), channel_id=1, source_target_pairs={{4,0},{8,4},{12,8},{16,12},{20,16},{24,20},{28,24},{0,28},{5,1},{9... | collective-permute-start | bytes 24584 | tf_op jit(solution)/shard_map/ppermute | solution.py:24
  146.8 1.8 collective-permute-done.47
  153.3 4.8 %collective-permute-start.49 = (f32[3,16,512]{2,1,0:T(8,128)S(1)}, f32[3,16,512]{2,1,0:T(8,128)S(1)}, u32[]{:S(2)}, u32[]{:S(2)}) collective-permute-start(f32[3,16,512]{2,1,0:T(8,128)S(1)} %get-tuple-element.93), channel_id=1, source_target_pairs={{4,0},{8,4},{12,8},{16,12},{20,16},{24,20},{28,24},{0,28},{5,1},{9... | collective-permute-start | bytes 294920 | tf_op jit(solution)/shard_map/ppermute | solution.py:24
  158.1 2.5 collective-permute-done.48
  162.5 2.1 collective-permute-done.50
  167.2 4.8 %collective-permute-start.52 = (f32[1,16,512]{2,1,0:T(8,128)S(1)}, f32[1,16,512]{2,1,0:T(8,128)S(1)}, u32[]{:S(2)}, u32[]{:S(2)}) collective-permute-start(f32[1,16,512]{2,1,0:T(8,128)S(1)} %get-tuple-element.91), channel_id=1, source_target_pairs={{4,0},{8,4},{12,8},{16,12},{20,16},{24,20},{28,24},{0,28},{5,1},{9... | collective-permute-start | bytes 98312 | tf_op jit(solution)/shard_map/ppermute | solution.py:24
  172.0 1.8 collective-permute-done.53
  178.1 5.0 %collective-permute-start.57 = (f32[3,16,512]{2,1,0:T(8,128)S(1)}, f32[3,16,512]{2,1,0:T(8,128)S(1)}, u32[]{:S(2)}, u32[]{:S(2)}) collective-permute-start(f32[3,16,512]{2,1,0:T(8,128)S(1)} %get-tuple-element.89), channel_id=1, source_target_pairs={{4,0},{8,4},{12,8},{16,12},{20,16},{24,20},{28,24},{0,28},{5,1},{9... | collective-permute-start | bytes 294920 | tf_op jit(solution)/shard_map/ppermute | solution.py:24
  183.2 2.5 collective-permute-done.56
  187.5 2.1 collective-permute-done.58
  190.7 4.8 %collective-permute-start.60 = (f32[1,16,512]{2,1,0:T(8,128)S(1)}, f32[1,16,512]{2,1,0:T(8,128)S(1)}, u32[]{:S(2)}, u32[]{:S(2)}) collective-permute-start(f32[1,16,512]{2,1,0:T(8,128)S(1)} %get-tuple-element.87), channel_id=1, source_target_pairs={{4,0},{8,4},{12,8},{16,12},{20,16},{24,20},{28,24},{0,28},{5,1},{9... | collective-permute-start | bytes 98312 | tf_op jit(solution)/shard_map/ppermute | solution.py:24
  195.5 1.9 collective-permute-done.61
  201.6 9.8 %reshape.198 = f32[2,2,8,2,256,2]{5,4,3,2,1,0:T(8,128)} reshape(f32[4,16,512]{2,1,0:T(8,128)S(1)} %fusion.103) | data formatting | bytes 262144 | tf_op jit(solution)/shard_map/reshape | solution.py:86
  211.4 4.0 %reduce_sum.83 = f32[2,8,256]{2,1,0:T(8,128)S(1)} reduce(f32[2,2,8,2,256,2]{5,4,3,2,1,0:T(8,128)} %reshape.198, f32[]{:T(128)} %constant.27.clone.1), dimensions={1,3,5}, to_apply=%region_6.7 | reduce | flops 28672 | bytes 147460 | tf_op jit(solution)/shard_map/reduce_sum | solution.py:86
  215.5 4.7 %collective-permute-start.64 = (f32[1,8,256]{2,1,0:T(8,128)S(1)}, f32[1,8,256]{2,1,0:T(8,128)S(1)}, u32[]{:S(2)}, u32[]{:S(2)}) collective-permute-start(f32[1,8,256]{2,1,0:T(8,128)S(1)} %get-tuple-element.135), channel_id=1, source_target_pairs={{4,0},{8,4},{12,8},{16,12},{20,16},{24,20},{28,24},{0,28},{5,1},{9... | collective-permute-start | bytes 24584 | tf_op jit(solution)/shard_map/ppermute | solution.py:24
  223.2 1.8 collective-permute-done.67
  225.1 4.8 %collective-permute-start.68 = (f32[1,8,256]{2,1,0:T(8,128)S(1)}, f32[1,8,256]{2,1,0:T(8,128)S(1)}, u32[]{:S(2)}, u32[]{:S(2)}) collective-permute-start(f32[1,8,256]{2,1,0:T(8,128)S(1)} %get-tuple-element.133), channel_id=1, source_target_pairs={{4,0},{8,4},{12,8},{16,12},{20,16},{24,20},{28,24},{0,28},{5,1},{9... | collective-permute-start | bytes 24584 | tf_op jit(solution)/shard_map/ppermute | solution.py:24
  232.9 1.8 collective-permute-done.71
  234.8 4.8 %collective-permute-start.72 = (f32[1,8,256]{2,1,0:T(8,128)S(1)}, f32[1,8,256]{2,1,0:T(8,128)S(1)}, u32[]{:S(2)}, u32[]{:S(2)}) collective-permute-start(f32[1,8,256]{2,1,0:T(8,128)S(1)} %get-tuple-element.131), channel_id=1, source_target_pairs={{4,0},{8,4},{12,8},{16,12},{20,16},{24,20},{28,24},{0,28},{5,1},{9... | collective-permute-start | bytes 24584 | tf_op jit(solution)/shard_map/ppermute | solution.py:24
  242.6 1.8 collective-permute-done.75
  245.1 4.8 %collective-permute-start.76 = (f32[1,4,128]{2,1,0:T(4,128)S(1)}, f32[1,4,128]{2,1,0:T(4,128)S(1)}, u32[]{:S(2)}, u32[]{:S(2)}) collective-permute-start(f32[1,4,128]{2,1,0:T(4,128)S(1)} %bitcast_multiply_fusion.3), channel_id=1, source_target_pairs={{4,0},{8,4},{12,8},{16,12},{20,16},{24,20},{28,24},{0,28},{5,1},{9... | collective-permute-start | bytes 6152 | tf_op jit(solution)/shard_map/ppermute | solution.py:24
  252.8 1.8 collective-permute-done.79
  254.7 4.8 %collective-permute-start.80 = (f32[1,4,128]{2,1,0:T(4,128)S(1)}, f32[1,4,128]{2,1,0:T(4,128)S(1)}, u32[]{:S(2)}, u32[]{:S(2)}) collective-permute-start(f32[1,4,128]{2,1,0:T(4,128)S(1)} %get-tuple-element.22), channel_id=1, source_target_pairs={{4,0},{8,4},{12,8},{16,12},{20,16},{24,20},{28,24},{0,28},{5,1},{9... | collective-permute-start | bytes 6152 | tf_op jit(solution)/shard_map/ppermute | solution.py:24
  262.3 1.8 collective-permute-done.83
  264.2 4.8 %collective-permute-start.84 = (f32[1,4,128]{2,1,0:T(4,128)S(1)}, f32[1,4,128]{2,1,0:T(4,128)S(1)}, u32[]{:S(2)}, u32[]{:S(2)}) collective-permute-start(f32[1,4,128]{2,1,0:T(4,128)S(1)} %get-tuple-element.20), channel_id=1, source_target_pairs={{4,0},{8,4},{12,8},{16,12},{20,16},{24,20},{28,24},{0,28},{5,1},{9... | collective-permute-start | bytes 6152 | tf_op jit(solution)/shard_map/ppermute | solution.py:24
  271.8 1.8 collective-permute-done.87
  274.0 4.8 %collective-permute-start.88 = (f32[1,8,256]{2,1,0:T(8,128)S(1)}, f32[1,8,256]{2,1,0:T(8,128)S(1)}, u32[]{:S(2)}, u32[]{:S(2)}) collective-permute-start(f32[1,8,256]{2,1,0:T(8,128)S(1)} %get-tuple-element.129), channel_id=1, source_target_pairs={{4,0},{8,4},{12,8},{16,12},{20,16},{24,20},{28,24},{0,28},{5,1},{9... | collective-permute-start | bytes 24584 | tf_op jit(solution)/shard_map/ppermute | solution.py:24
  281.7 1.8 collective-permute-done.91
  283.7 4.8 %collective-permute-start.92 = (f32[1,8,256]{2,1,0:T(8,128)S(1)}, f32[1,8,256]{2,1,0:T(8,128)S(1)}, u32[]{:S(2)}, u32[]{:S(2)}) collective-permute-start(f32[1,8,256]{2,1,0:T(8,128)S(1)} %get-tuple-element.127), channel_id=1, source_target_pairs={{4,0},{8,4},{12,8},{16,12},{20,16},{24,20},{28,24},{0,28},{5,1},{9... | collective-permute-start | bytes 24584 | tf_op jit(solution)/shard_map/ppermute | solution.py:24
  291.4 1.8 collective-permute-done.95
  293.4 4.8 %collective-permute-start.96 = (f32[1,8,256]{2,1,0:T(8,128)S(1)}, f32[1,8,256]{2,1,0:T(8,128)S(1)}, u32[]{:S(2)}, u32[]{:S(2)}) collective-permute-start(f32[1,8,256]{2,1,0:T(8,128)S(1)} %get-tuple-element.125), channel_id=1, source_target_pairs={{4,0},{8,4},{12,8},{16,12},{20,16},{24,20},{28,24},{0,28},{5,1},{9... | collective-permute-start | bytes 24584 | tf_op jit(solution)/shard_map/ppermute | solution.py:24
  301.4 1.8 collective-permute-done.99
  307.7 4.8 %collective-permute-start.101 = (f32[3,16,512]{2,1,0:T(8,128)S(1)}, f32[3,16,512]{2,1,0:T(8,128)S(1)}, u32[]{:S(2)}, u32[]{:S(2)}) collective-permute-start(f32[3,16,512]{2,1,0:T(8,128)S(1)} %get-tuple-element.85), channel_id=1, source_target_pairs={{4,0},{8,4},{12,8},{16,12},{20,16},{24,20},{28,24},{0,28},{5,1},{9... | collective-permute-start | bytes 294920 | tf_op jit(solution)/shard_map/ppermute | solution.py:24
  312.6 2.5 collective-permute-done.100
  316.9 2.1 collective-permute-done.102
  321.7 4.8 %collective-permute-start.104 = (f32[1,16,512]{2,1,0:T(8,128)S(1)}, f32[1,16,512]{2,1,0:T(8,128)S(1)}, u32[]{:S(2)}, u32[]{:S(2)}) collective-permute-start(f32[1,16,512]{2,1,0:T(8,128)S(1)} %get-tuple-element.83), channel_id=1, source_target_pairs={{4,0},{8,4},{12,8},{16,12},{20,16},{24,20},{28,24},{0,28},{5,1},{9... | collective-permute-start | bytes 98312 | tf_op jit(solution)/shard_map/ppermute | solution.py:24
  326.5 1.8 collective-permute-done.105
  (314 shorter events, 102.7 us)
Async XLA Ops:
  1.7 11.8 %collective-permute-start = (f32[3,16,512]{2,1,0:T(8,128)S(1)}, f32[3,16,512]{2,1,0:T(8,128)S(1)}, u32[]{:S(2)}, u32[]{:S(2)}) collective-permute-start(f32[3,16,512]{2,1,0:T(8,128)S(1)} %get-tuple-element.99), channel_id=1, source_target_pairs={{0,4},{4,8},{8,12},{12,16},{16,20},{20,24},{24,28},{28,0},{1,5},{5... | collective-permute-start | bytes 294920 | tf_op jit(solution)/shard_map/ppermute | solution.py:23
  5.7 13.4 %collective-permute-start.5 = (f32[3,16,512]{2,1,0:T(8,128)S(1)}, f32[3,16,512]{2,1,0:T(8,128)S(1)}, u32[]{:S(2)}, u32[]{:S(2)}) collective-permute-start(f32[3,16,512]{2,1,0:T(8,128)S(1)} %get-tuple-element.96), channel_id=1, source_target_pairs={{4,0},{8,4},{12,8},{16,12},{20,16},{24,20},{28,24},{0,28},{5,1},{9... | collective-permute-start | bytes 294920 | tf_op jit(solution)/shard_map/ppermute | solution.py:24
  8.8 9.4 %collective-permute-start.4 = (f32[3,16,512]{2,1,0:T(8,128)S(1)}, f32[3,16,512]{2,1,0:T(8,128)S(1)}, u32[]{:S(2)}, u32[]{:S(2)}) collective-permute-start(f32[3,16,512]{2,1,0:T(8,128)S(1)} %get-tuple-element.97), channel_id=1, source_target_pairs={{0,4},{4,8},{8,12},{12,16},{16,20},{20,24},{24,28},{28,0},{1,5},{5... | collective-permute-start | bytes 294920 | tf_op jit(solution)/shard_map/ppermute | solution.py:23
  8.8 7.5 %collective-permute-start.1 = (f32[3,16,512]{2,1,0:T(8,128)S(1)}, f32[3,16,512]{2,1,0:T(8,128)S(1)}, u32[]{:S(2)}, u32[]{:S(2)}) collective-permute-start(f32[3,16,512]{2,1,0:T(8,128)S(1)} %get-tuple-element.98), channel_id=1, source_target_pairs={{4,0},{8,4},{12,8},{16,12},{20,16},{24,20},{28,24},{0,28},{5,1},{9... | collective-permute-start | bytes 294920 | tf_op jit(solution)/shard_map/ppermute | solution.py:24
  16.4 4.6 %collective-permute-start.2 = (f32[10,3,512]{2,1,0:T(4,128)S(1)}, f32[10,3,512]{2,1,0:T(4,128)S(1)}, u32[]{:S(2)}, u32[]{:S(2)}) collective-permute-start(f32[10,3,512]{2,1,0:T(4,128)S(1)} %get-tuple-element.72), channel_id=1, source_target_pairs={{0,1},{1,2},{2,3},{3,0},{4,5},{5,6},{6,7},{7,4},{8,9},{9,10},{10,1... | collective-permute-start | bytes 184328 | tf_op jit(solution)/shard_map/ppermute | solution.py:23
  16.4 4.5 %collective-permute-start.3 = (f32[10,3,512]{2,1,0:T(4,128)S(1)}, f32[10,3,512]{2,1,0:T(4,128)S(1)}, u32[]{:S(2)}, u32[]{:S(2)}) collective-permute-start(f32[10,3,512]{2,1,0:T(4,128)S(1)} %get-tuple-element.73), channel_id=1, source_target_pairs={{1,0},{2,1},{3,2},{0,3},{5,4},{6,5},{7,6},{4,7},{9,8},{10,9},{11,1... | collective-permute-start | bytes 184328 | tf_op jit(solution)/shard_map/ppermute | solution.py:24
  19.2 3.9 %collective-permute-start.6 = (f32[10,3,512]{2,1,0:T(4,128)S(1)}, f32[10,3,512]{2,1,0:T(4,128)S(1)}, u32[]{:S(2)}, u32[]{:S(2)}) collective-permute-start(f32[10,3,512]{2,1,0:T(4,128)S(1)} %get-tuple-element.70), channel_id=1, source_target_pairs={{0,1},{1,2},{2,3},{3,0},{4,5},{5,6},{6,7},{7,4},{8,9},{9,10},{10,1... | collective-permute-start | bytes 184328 | tf_op jit(solution)/shard_map/ppermute | solution.py:23
  19.2 3.9 %collective-permute-start.7 = (f32[10,3,512]{2,1,0:T(4,128)S(1)}, f32[10,3,512]{2,1,0:T(4,128)S(1)}, u32[]{:S(2)}, u32[]{:S(2)}) collective-permute-start(f32[10,3,512]{2,1,0:T(4,128)S(1)} %get-tuple-element.71), channel_id=1, source_target_pairs={{1,0},{2,1},{3,2},{0,3},{5,4},{6,5},{7,6},{4,7},{9,8},{10,9},{11,1... | collective-permute-start | bytes 184328 | tf_op jit(solution)/shard_map/ppermute | solution.py:24
  24.5 6.7 %collective-permute-start.9 = (f32[1,16,512]{2,1,0:T(8,128)S(1)}, f32[1,16,512]{2,1,0:T(8,128)S(1)}, u32[]{:S(2)}, u32[]{:S(2)}) collective-permute-start(f32[1,16,512]{2,1,0:T(8,128)S(1)} %get-tuple-element.94), channel_id=1, source_target_pairs={{0,4},{4,8},{8,12},{12,16},{16,20},{20,24},{24,28},{28,0},{1,5},{5... | collective-permute-start | bytes 98312 | tf_op jit(solution)/shard_map/ppermute | solution.py:23
  24.5 6.6 %collective-permute-start.8 = (f32[1,16,512]{2,1,0:T(8,128)S(1)}, f32[1,16,512]{2,1,0:T(8,128)S(1)}, u32[]{:S(2)}, u32[]{:S(2)}) collective-permute-start(f32[1,16,512]{2,1,0:T(8,128)S(1)} %get-tuple-element.95), channel_id=1, source_target_pairs={{4,0},{8,4},{12,8},{16,12},{20,16},{24,20},{28,24},{0,28},{5,1},{9... | collective-permute-start | bytes 98312 | tf_op jit(solution)/shard_map/ppermute | solution.py:24
  31.1 15.1 %collective-permute-start.10 = (f32[6,1,512]{2,1,0:T(1,128)S(1)}, f32[6,1,512]{2,1,0:T(1,128)S(1)}, u32[]{:S(2)}, u32[]{:S(2)}) collective-permute-start(f32[6,1,512]{2,1,0:T(1,128)S(1)} %get-tuple-element.80), channel_id=1, source_target_pairs={{1,0},{2,1},{3,2},{0,3},{5,4},{6,5},{7,6},{4,7},{9,8},{10,9},{11,1... | collective-permute-start | bytes 36872 | tf_op jit(solution)/shard_map/ppermute | solution.py:24
  32.5 13.8 %collective-permute-start.11 = (f32[6,1,512]{2,1,0:T(1,128)S(1)}, f32[6,1,512]{2,1,0:T(1,128)S(1)}, u32[]{:S(2)}, u32[]{:S(2)}) collective-permute-start(f32[6,1,512]{2,1,0:T(1,128)S(1)} %get-tuple-element.81), channel_id=1, source_target_pairs={{0,1},{1,2},{2,3},{3,0},{4,5},{5,6},{6,7},{7,4},{8,9},{9,10},{10,1... | collective-permute-start | bytes 36872 | tf_op jit(solution)/shard_map/ppermute | solution.py:23
  60.3 6.4 %collective-permute-start.13 = (f32[1,8,256]{2,1,0:T(8,128)S(1)}, f32[1,8,256]{2,1,0:T(8,128)S(1)}, u32[]{:S(2)}, u32[]{:S(2)}) collective-permute-start(f32[1,8,256]{2,1,0:T(8,128)S(1)} %get-tuple-element.148), channel_id=1, source_target_pairs={{0,4},{4,8},{8,12},{12,16},{16,20},{20,24},{24,28},{28,0},{1,5},{5... | collective-permute-start | bytes 24584 | tf_op jit(solution)/shard_map/ppermute | solution.py:23
  60.3 6.3 %collective-permute-start.12 = (f32[1,8,256]{2,1,0:T(8,128)S(1)}, f32[1,8,256]{2,1,0:T(8,128)S(1)}, u32[]{:S(2)}, u32[]{:S(2)}) collective-permute-start(f32[1,8,256]{2,1,0:T(8,128)S(1)} %get-tuple-element.149), channel_id=1, source_target_pairs={{4,0},{8,4},{12,8},{16,12},{20,16},{24,20},{28,24},{0,28},{5,1},{9... | collective-permute-start | bytes 24584 | tf_op jit(solution)/shard_map/ppermute | solution.py:24
  70.6 6.4 %collective-permute-start.17 = (f32[1,8,256]{2,1,0:T(8,128)S(1)}, f32[1,8,256]{2,1,0:T(8,128)S(1)}, u32[]{:S(2)}, u32[]{:S(2)}) collective-permute-start(f32[1,8,256]{2,1,0:T(8,128)S(1)} %get-tuple-element.146), channel_id=1, source_target_pairs={{0,4},{4,8},{8,12},{12,16},{16,20},{20,24},{24,28},{28,0},{1,5},{5... | collective-permute-start | bytes 24584 | tf_op jit(solution)/shard_map/ppermute | solution.py:23
  70.7 6.3 %collective-permute-start.16 = (f32[1,8,256]{2,1,0:T(8,128)S(1)}, f32[1,8,256]{2,1,0:T(8,128)S(1)}, u32[]{:S(2)}, u32[]{:S(2)}) collective-permute-start(f32[1,8,256]{2,1,0:T(8,128)S(1)} %get-tuple-element.147), channel_id=1, source_target_pairs={{4,0},{8,4},{12,8},{16,12},{20,16},{24,20},{28,24},{0,28},{5,1},{9... | collective-permute-start | bytes 24584 | tf_op jit(solution)/shard_map/ppermute | solution.py:24
  80.3 6.4 %collective-permute-start.21 = (f32[1,8,256]{2,1,0:T(8,128)S(1)}, f32[1,8,256]{2,1,0:T(8,128)S(1)}, u32[]{:S(2)}, u32[]{:S(2)}) collective-permute-start(f32[1,8,256]{2,1,0:T(8,128)S(1)} %get-tuple-element.142), channel_id=1, source_target_pairs={{0,4},{4,8},{8,12},{12,16},{16,20},{20,24},{24,28},{28,0},{1,5},{5... | collective-permute-start | bytes 24584 | tf_op jit(solution)/shard_map/ppermute | solution.py:23
  80.4 6.3 %collective-permute-start.20 = (f32[1,8,256]{2,1,0:T(8,128)S(1)}, f32[1,8,256]{2,1,0:T(8,128)S(1)}, u32[]{:S(2)}, u32[]{:S(2)}) collective-permute-start(f32[1,8,256]{2,1,0:T(8,128)S(1)} %get-tuple-element.143), channel_id=1, source_target_pairs={{4,0},{8,4},{12,8},{16,12},{20,16},{24,20},{28,24},{0,28},{5,1},{9... | collective-permute-start | bytes 24584 | tf_op jit(solution)/shard_map/ppermute | solution.py:24
  90.6 6.4 %collective-permute-start.25 = (f32[1,4,128]{2,1,0:T(4,128)S(1)}, f32[1,4,128]{2,1,0:T(4,128)S(1)}, u32[]{:S(2)}, u32[]{:S(2)}) collective-permute-start(f32[1,4,128]{2,1,0:T(4,128)S(1)} %bitcast_multiply_fusion.6), channel_id=1, source_target_pairs={{0,4},{4,8},{8,12},{12,16},{16,20},{20,24},{24,28},{28,0},{1,5},{5... | collective-permute-start | bytes 6152 | tf_op jit(solution)/shard_map/ppermute | solution.py:23
  90.7 6.3 %collective-permute-start.24 = (f32[1,4,128]{2,1,0:T(4,128)S(1)}, f32[1,4,128]{2,1,0:T(4,128)S(1)}, u32[]{:S(2)}, u32[]{:S(2)}) collective-permute-start(f32[1,4,128]{2,1,0:T(4,128)S(1)} %bitcast_multiply_fusion.6), channel_id=1, source_target_pairs={{4,0},{8,4},{12,8},{16,12},{20,16},{24,20},{28,24},{0,28},{5,1},{9... | collective-permute-start | bytes 6152 | tf_op jit(solution)/shard_map/ppermute | solution.py:24
  100.2 6.3 %collective-permute-start.29 = (f32[1,4,128]{2,1,0:T(4,128)S(1)}, f32[1,4,128]{2,1,0:T(4,128)S(1)}, u32[]{:S(2)}, u32[]{:S(2)}) collective-permute-start(f32[1,4,128]{2,1,0:T(4,128)S(1)} %get-tuple-element.45), channel_id=1, source_target_pairs={{0,4},{4,8},{8,12},{12,16},{16,20},{20,24},{24,28},{28,0},{1,5},{5... | collective-permute-start | bytes 6152 | tf_op jit(solution)/shard_map/ppermute | solution.py:23
  100.2 6.3 %collective-permute-start.28 = (f32[1,4,128]{2,1,0:T(4,128)S(1)}, f32[1,4,128]{2,1,0:T(4,128)S(1)}, u32[]{:S(2)}, u32[]{:S(2)}) collective-permute-start(f32[1,4,128]{2,1,0:T(4,128)S(1)} %get-tuple-element.45), channel_id=1, source_target_pairs={{4,0},{8,4},{12,8},{16,12},{20,16},{24,20},{28,24},{0,28},{5,1},{9... | collective-permute-start | bytes 6152 | tf_op jit(solution)/shard_map/ppermute | solution.py:24
  109.7 6.3 %collective-permute-start.33 = (f32[1,4,128]{2,1,0:T(4,128)S(1)}, f32[1,4,128]{2,1,0:T(4,128)S(1)}, u32[]{:S(2)}, u32[]{:S(2)}) collective-permute-start(f32[1,4,128]{2,1,0:T(4,128)S(1)} %get-tuple-element.43), channel_id=1, source_target_pairs={{0,4},{4,8},{8,12},{12,16},{16,20},{20,24},{24,28},{28,0},{1,5},{5... | collective-permute-start | bytes 6152 | tf_op jit(solution)/shard_map/ppermute | solution.py:23
  109.7 6.3 %collective-permute-start.32 = (f32[1,4,128]{2,1,0:T(4,128)S(1)}, f32[1,4,128]{2,1,0:T(4,128)S(1)}, u32[]{:S(2)}, u32[]{:S(2)}) collective-permute-start(f32[1,4,128]{2,1,0:T(4,128)S(1)} %get-tuple-element.43), channel_id=1, source_target_pairs={{4,0},{8,4},{12,8},{16,12},{20,16},{24,20},{28,24},{0,28},{5,1},{9... | collective-permute-start | bytes 6152 | tf_op jit(solution)/shard_map/ppermute | solution.py:24
  119.4 6.4 %collective-permute-start.37 = (f32[1,8,256]{2,1,0:T(8,128)S(1)}, f32[1,8,256]{2,1,0:T(8,128)S(1)}, u32[]{:S(2)}, u32[]{:S(2)}) collective-permute-start(f32[1,8,256]{2,1,0:T(8,128)S(1)} %get-tuple-element.140), channel_id=1, source_target_pairs={{0,4},{4,8},{8,12},{12,16},{16,20},{20,24},{24,28},{28,0},{1,5},{5... | collective-permute-start | bytes 24584 | tf_op jit(solution)/shard_map/ppermute | solution.py:23
  119.5 6.3 %collective-permute-start.36 = (f32[1,8,256]{2,1,0:T(8,128)S(1)}, f32[1,8,256]{2,1,0:T(8,128)S(1)}, u32[]{:S(2)}, u32[]{:S(2)}) collective-permute-start(f32[1,8,256]{2,1,0:T(8,128)S(1)} %get-tuple-element.141), channel_id=1, source_target_pairs={{4,0},{8,4},{12,8},{16,12},{20,16},{24,20},{28,24},{0,28},{5,1},{9... | collective-permute-start | bytes 24584 | tf_op jit(solution)/shard_map/ppermute | solution.py:24
  129.1 6.4 %collective-permute-start.41 = (f32[1,8,256]{2,1,0:T(8,128)S(1)}, f32[1,8,256]{2,1,0:T(8,128)S(1)}, u32[]{:S(2)}, u32[]{:S(2)}) collective-permute-start(f32[1,8,256]{2,1,0:T(8,128)S(1)} %get-tuple-element.138), channel_id=1, source_target_pairs={{0,4},{4,8},{8,12},{12,16},{16,20},{20,24},{24,28},{28,0},{1,5},{5... | collective-permute-start | bytes 24584 | tf_op jit(solution)/shard_map/ppermute | solution.py:23
  129.2 6.4 %collective-permute-start.40 = (f32[1,8,256]{2,1,0:T(8,128)S(1)}, f32[1,8,256]{2,1,0:T(8,128)S(1)}, u32[]{:S(2)}, u32[]{:S(2)}) collective-permute-start(f32[1,8,256]{2,1,0:T(8,128)S(1)} %get-tuple-element.139), channel_id=1, source_target_pairs={{4,0},{8,4},{12,8},{16,12},{20,16},{24,20},{28,24},{0,28},{5,1},{9... | collective-permute-start | bytes 24584 | tf_op jit(solution)/shard_map/ppermute | solution.py:24
  138.8 6.5 %collective-permute-start.45 = (f32[1,8,256]{2,1,0:T(8,128)S(1)}, f32[1,8,256]{2,1,0:T(8,128)S(1)}, u32[]{:S(2)}, u32[]{:S(2)}) collective-permute-start(f32[1,8,256]{2,1,0:T(8,128)S(1)} %get-tuple-element.136), channel_id=1, source_target_pairs={{0,4},{4,8},{8,12},{12,16},{16,20},{20,24},{24,28},{28,0},{1,5},{5... | collective-permute-start | bytes 24584 | tf_op jit(solution)/shard_map/ppermute | solution.py:23
  138.9 6.4 %collective-permute-start.44 = (f32[1,8,256]{2,1,0:T(8,128)S(1)}, f32[1,8,256]{2,1,0:T(8,128)S(1)}, u32[]{:S(2)}, u32[]{:S(2)}) collective-permute-start(f32[1,8,256]{2,1,0:T(8,128)S(1)} %get-tuple-element.137), channel_id=1, source_target_pairs={{4,0},{8,4},{12,8},{16,12},{20,16},{24,20},{28,24},{0,28},{5,1},{9... | collective-permute-start | bytes 24584 | tf_op jit(solution)/shard_map/ppermute | solution.py:24
  153.2 7.4 %collective-permute-start.48 = (f32[3,16,512]{2,1,0:T(8,128)S(1)}, f32[3,16,512]{2,1,0:T(8,128)S(1)}, u32[]{:S(2)}, u32[]{:S(2)}) collective-permute-start(f32[3,16,512]{2,1,0:T(8,128)S(1)} %get-tuple-element.92), channel_id=1, source_target_pairs={{0,4},{4,8},{8,12},{12,16},{16,20},{20,24},{24,28},{28,0},{1,5},{5... | collective-permute-start | bytes 294920 | tf_op jit(solution)/shard_map/ppermute | solution.py:23
  153.3 7.4 %collective-permute-start.49 = (f32[3,16,512]{2,1,0:T(8,128)S(1)}, f32[3,16,512]{2,1,0:T(8,128)S(1)}, u32[]{:S(2)}, u32[]{:S(2)}) collective-permute-start(f32[3,16,512]{2,1,0:T(8,128)S(1)} %get-tuple-element.93), channel_id=1, source_target_pairs={{4,0},{8,4},{12,8},{16,12},{20,16},{24,20},{28,24},{0,28},{5,1},{9... | collective-permute-start | bytes 294920 | tf_op jit(solution)/shard_map/ppermute | solution.py:24
  160.7 3.9 %collective-permute-start.50 = (f32[10,3,512]{2,1,0:T(4,128)S(1)}, f32[10,3,512]{2,1,0:T(4,128)S(1)}, u32[]{:S(2)}, u32[]{:S(2)}) collective-permute-start(f32[10,3,512]{2,1,0:T(4,128)S(1)} %get-tuple-element.68), channel_id=1, source_target_pairs={{0,1},{1,2},{2,3},{3,0},{4,5},{5,6},{6,7},{7,4},{8,9},{9,10},{10,1... | collective-permute-start | bytes 184328 | tf_op jit(solution)/shard_map/ppermute | solution.py:23
  167.1 6.7 %collective-permute-start.53 = (f32[1,16,512]{2,1,0:T(8,128)S(1)}, f32[1,16,512]{2,1,0:T(8,128)S(1)}, u32[]{:S(2)}, u32[]{:S(2)}) collective-permute-start(f32[1,16,512]{2,1,0:T(8,128)S(1)} %get-tuple-element.90), channel_id=1, source_target_pairs={{0,4},{4,8},{8,12},{12,16},{16,20},{20,24},{24,28},{28,0},{1,5},{5... | collective-permute-start | bytes 98312 | tf_op jit(solution)/shard_map/ppermute | solution.py:23
  167.2 6.7 %collective-permute-start.52 = (f32[1,16,512]{2,1,0:T(8,128)S(1)}, f32[1,16,512]{2,1,0:T(8,128)S(1)}, u32[]{:S(2)}, u32[]{:S(2)}) collective-permute-start(f32[1,16,512]{2,1,0:T(8,128)S(1)} %get-tuple-element.91), channel_id=1, source_target_pairs={{4,0},{8,4},{12,8},{16,12},{20,16},{24,20},{28,24},{0,28},{5,1},{9... | collective-permute-start | bytes 98312 | tf_op jit(solution)/shard_map/ppermute | solution.py:24
  178.1 7.6 %collective-permute-start.56 = (f32[3,16,512]{2,1,0:T(8,128)S(1)}, f32[3,16,512]{2,1,0:T(8,128)S(1)}, u32[]{:S(2)}, u32[]{:S(2)}) collective-permute-start(f32[3,16,512]{2,1,0:T(8,128)S(1)} %get-tuple-element.88), channel_id=1, source_target_pairs={{0,4},{4,8},{8,12},{12,16},{16,20},{20,24},{24,28},{28,0},{1,5},{5... | collective-permute-start | bytes 294920 | tf_op jit(solution)/shard_map/ppermute | solution.py:23
  178.1 7.6 %collective-permute-start.57 = (f32[3,16,512]{2,1,0:T(8,128)S(1)}, f32[3,16,512]{2,1,0:T(8,128)S(1)}, u32[]{:S(2)}, u32[]{:S(2)}) collective-permute-start(f32[3,16,512]{2,1,0:T(8,128)S(1)} %get-tuple-element.89), channel_id=1, source_target_pairs={{4,0},{8,4},{12,8},{16,12},{20,16},{24,20},{28,24},{0,28},{5,1},{9... | collective-permute-start | bytes 294920 | tf_op jit(solution)/shard_map/ppermute | solution.py:24
  185.7 3.9 %collective-permute-start.58 = (f32[10,3,512]{2,1,0:T(4,128)S(1)}, f32[10,3,512]{2,1,0:T(4,128)S(1)}, u32[]{:S(2)}, u32[]{:S(2)}) collective-permute-start(f32[10,3,512]{2,1,0:T(4,128)S(1)} %get-tuple-element.66), channel_id=1, source_target_pairs={{0,1},{1,2},{2,3},{3,0},{4,5},{5,6},{6,7},{7,4},{8,9},{9,10},{10,1... | collective-permute-start | bytes 184328 | tf_op jit(solution)/shard_map/ppermute | solution.py:23
  185.8 3.9 %collective-permute-start.59 = (f32[10,3,512]{2,1,0:T(4,128)S(1)}, f32[10,3,512]{2,1,0:T(4,128)S(1)}, u32[]{:S(2)}, u32[]{:S(2)}) collective-permute-start(f32[10,3,512]{2,1,0:T(4,128)S(1)} %get-tuple-element.67), channel_id=1, source_target_pairs={{1,0},{2,1},{3,2},{0,3},{5,4},{6,5},{7,6},{4,7},{9,8},{10,9},{11,1... | collective-permute-start | bytes 184328 | tf_op jit(solution)/shard_map/ppermute | solution.py:24
  190.6 6.8 %collective-permute-start.61 = (f32[1,16,512]{2,1,0:T(8,128)S(1)}, f32[1,16,512]{2,1,0:T(8,128)S(1)}, u32[]{:S(2)}, u32[]{:S(2)}) collective-permute-start(f32[1,16,512]{2,1,0:T(8,128)S(1)} %get-tuple-element.86), channel_id=1, source_target_pairs={{0,4},{4,8},{8,12},{12,16},{16,20},{20,24},{24,28},{28,0},{1,5},{5... | collective-permute-start | bytes 98312 | tf_op jit(solution)/shard_map/ppermute | solution.py:23
  190.7 6.8 %collective-permute-start.60 = (f32[1,16,512]{2,1,0:T(8,128)S(1)}, f32[1,16,512]{2,1,0:T(8,128)S(1)}, u32[]{:S(2)}, u32[]{:S(2)}) collective-permute-start(f32[1,16,512]{2,1,0:T(8,128)S(1)} %get-tuple-element.87), channel_id=1, source_target_pairs={{4,0},{8,4},{12,8},{16,12},{20,16},{24,20},{28,24},{0,28},{5,1},{9... | collective-permute-start | bytes 98312 | tf_op jit(solution)/shard_map/ppermute | solution.py:24
  215.4 6.4 %collective-permute-start.65 = (f32[1,8,256]{2,1,0:T(8,128)S(1)}, f32[1,8,256]{2,1,0:T(8,128)S(1)}, u32[]{:S(2)}, u32[]{:S(2)}) collective-permute-start(f32[1,8,256]{2,1,0:T(8,128)S(1)} %get-tuple-element.134), channel_id=1, source_target_pairs={{0,4},{4,8},{8,12},{12,16},{16,20},{20,24},{24,28},{28,0},{1,5},{5... | collective-permute-start | bytes 24584 | tf_op jit(solution)/shard_map/ppermute | solution.py:23
  215.5 6.3 %collective-permute-start.64 = (f32[1,8,256]{2,1,0:T(8,128)S(1)}, f32[1,8,256]{2,1,0:T(8,128)S(1)}, u32[]{:S(2)}, u32[]{:S(2)}) collective-permute-start(f32[1,8,256]{2,1,0:T(8,128)S(1)} %get-tuple-element.135), channel_id=1, source_target_pairs={{4,0},{8,4},{12,8},{16,12},{20,16},{24,20},{28,24},{0,28},{5,1},{9... | collective-permute-start | bytes 24584 | tf_op jit(solution)/shard_map/ppermute | solution.py:24
  225.1 6.4 %collective-permute-start.69 = (f32[1,8,256]{2,1,0:T(8,128)S(1)}, f32[1,8,256]{2,1,0:T(8,128)S(1)}, u32[]{:S(2)}, u32[]{:S(2)}) collective-permute-start(f32[1,8,256]{2,1,0:T(8,128)S(1)} %get-tuple-element.132), channel_id=1, source_target_pairs={{0,4},{4,8},{8,12},{12,16},{16,20},{20,24},{24,28},{28,0},{1,5},{5... | collective-permute-start | bytes 24584 | tf_op jit(solution)/shard_map/ppermute | solution.py:23
  225.1 6.3 %collective-permute-start.68 = (f32[1,8,256]{2,1,0:T(8,128)S(1)}, f32[1,8,256]{2,1,0:T(8,128)S(1)}, u32[]{:S(2)}, u32[]{:S(2)}) collective-permute-start(f32[1,8,256]{2,1,0:T(8,128)S(1)} %get-tuple-element.133), channel_id=1, source_target_pairs={{4,0},{8,4},{12,8},{16,12},{20,16},{24,20},{28,24},{0,28},{5,1},{9... | collective-permute-start | bytes 24584 | tf_op jit(solution)/shard_map/ppermute | solution.py:24
  234.7 6.5 %collective-permute-start.73 = (f32[1,8,256]{2,1,0:T(8,128)S(1)}, f32[1,8,256]{2,1,0:T(8,128)S(1)}, u32[]{:S(2)}, u32[]{:S(2)}) collective-permute-start(f32[1,8,256]{2,1,0:T(8,128)S(1)} %get-tuple-element.130), channel_id=1, source_target_pairs={{0,4},{4,8},{8,12},{12,16},{16,20},{20,24},{24,28},{28,0},{1,5},{5... | collective-permute-start | bytes 24584 | tf_op jit(solution)/shard_map/ppermute | solution.py:23
  234.8 6.4 %collective-permute-start.72 = (f32[1,8,256]{2,1,0:T(8,128)S(1)}, f32[1,8,256]{2,1,0:T(8,128)S(1)}, u32[]{:S(2)}, u32[]{:S(2)}) collective-permute-start(f32[1,8,256]{2,1,0:T(8,128)S(1)} %get-tuple-element.131), channel_id=1, source_target_pairs={{4,0},{8,4},{12,8},{16,12},{20,16},{24,20},{28,24},{0,28},{5,1},{9... | collective-permute-start | bytes 24584 | tf_op jit(solution)/shard_map/ppermute | solution.py:24
  245.1 6.4 %collective-permute-start.77 = (f32[1,4,128]{2,1,0:T(4,128)S(1)}, f32[1,4,128]{2,1,0:T(4,128)S(1)}, u32[]{:S(2)}, u32[]{:S(2)}) collective-permute-start(f32[1,4,128]{2,1,0:T(4,128)S(1)} %bitcast_multiply_fusion.3), channel_id=1, source_target_pairs={{0,4},{4,8},{8,12},{12,16},{16,20},{20,24},{24,28},{28,0},{1,5},{5... | collective-permute-start | bytes 6152 | tf_op jit(solution)/shard_map/ppermute | solution.py:23
  245.1 6.3 %collective-permute-start.76 = (f32[1,4,128]{2,1,0:T(4,128)S(1)}, f32[1,4,128]{2,1,0:T(4,128)S(1)}, u32[]{:S(2)}, u32[]{:S(2)}) collective-permute-start(f32[1,4,128]{2,1,0:T(4,128)S(1)} %bitcast_multiply_fusion.3), channel_id=1, source_target_pairs={{4,0},{8,4},{12,8},{16,12},{20,16},{24,20},{28,24},{0,28},{5,1},{9... | collective-permute-start | bytes 6152 | tf_op jit(solution)/shard_map/ppermute | solution.py:24
  254.7 6.3 %collective-permute-start.81 = (f32[1,4,128]{2,1,0:T(4,128)S(1)}, f32[1,4,128]{2,1,0:T(4,128)S(1)}, u32[]{:S(2)}, u32[]{:S(2)}) collective-permute-start(f32[1,4,128]{2,1,0:T(4,128)S(1)} %get-tuple-element.22), channel_id=1, source_target_pairs={{0,4},{4,8},{8,12},{12,16},{16,20},{20,24},{24,28},{28,0},{1,5},{5... | collective-permute-start | bytes 6152 | tf_op jit(solution)/shard_map/ppermute | solution.py:23
  254.7 6.3 %collective-permute-start.80 = (f32[1,4,128]{2,1,0:T(4,128)S(1)}, f32[1,4,128]{2,1,0:T(4,128)S(1)}, u32[]{:S(2)}, u32[]{:S(2)}) collective-permute-start(f32[1,4,128]{2,1,0:T(4,128)S(1)} %get-tuple-element.22), channel_id=1, source_target_pairs={{4,0},{8,4},{12,8},{16,12},{20,16},{24,20},{28,24},{0,28},{5,1},{9... | collective-permute-start | bytes 6152 | tf_op jit(solution)/shard_map/ppermute | solution.py:24
  264.2 6.3 %collective-permute-start.85 = (f32[1,4,128]{2,1,0:T(4,128)S(1)}, f32[1,4,128]{2,1,0:T(4,128)S(1)}, u32[]{:S(2)}, u32[]{:S(2)}) collective-permute-start(f32[1,4,128]{2,1,0:T(4,128)S(1)} %get-tuple-element.20), channel_id=1, source_target_pairs={{0,4},{4,8},{8,12},{12,16},{16,20},{20,24},{24,28},{28,0},{1,5},{5... | collective-permute-start | bytes 6152 | tf_op jit(solution)/shard_map/ppermute | solution.py:23
  264.2 6.3 %collective-permute-start.84 = (f32[1,4,128]{2,1,0:T(4,128)S(1)}, f32[1,4,128]{2,1,0:T(4,128)S(1)}, u32[]{:S(2)}, u32[]{:S(2)}) collective-permute-start(f32[1,4,128]{2,1,0:T(4,128)S(1)} %get-tuple-element.20), channel_id=1, source_target_pairs={{4,0},{8,4},{12,8},{16,12},{20,16},{24,20},{28,24},{0,28},{5,1},{9... | collective-permute-start | bytes 6152 | tf_op jit(solution)/shard_map/ppermute | solution.py:24
  273.9 6.4 %collective-permute-start.89 = (f32[1,8,256]{2,1,0:T(8,128)S(1)}, f32[1,8,256]{2,1,0:T(8,128)S(1)}, u32[]{:S(2)}, u32[]{:S(2)}) collective-permute-start(f32[1,8,256]{2,1,0:T(8,128)S(1)} %get-tuple-element.128), channel_id=1, source_target_pairs={{0,4},{4,8},{8,12},{12,16},{16,20},{20,24},{24,28},{28,0},{1,5},{5... | collective-permute-start | bytes 24584 | tf_op jit(solution)/shard_map/ppermute | solution.py:23
  274.0 6.3 %collective-permute-start.88 = (f32[1,8,256]{2,1,0:T(8,128)S(1)}, f32[1,8,256]{2,1,0:T(8,128)S(1)}, u32[]{:S(2)}, u32[]{:S(2)}) collective-permute-start(f32[1,8,256]{2,1,0:T(8,128)S(1)} %get-tuple-element.129), channel_id=1, source_target_pairs={{4,0},{8,4},{12,8},{16,12},{20,16},{24,20},{28,24},{0,28},{5,1},{9... | collective-permute-start | bytes 24584 | tf_op jit(solution)/shard_map/ppermute | solution.py:24
  283.6 6.4 %collective-permute-start.93 = (f32[1,8,256]{2,1,0:T(8,128)S(1)}, f32[1,8,256]{2,1,0:T(8,128)S(1)}, u32[]{:S(2)}, u32[]{:S(2)}) collective-permute-start(f32[1,8,256]{2,1,0:T(8,128)S(1)} %get-tuple-element.126), channel_id=1, source_target_pairs={{0,4},{4,8},{8,12},{12,16},{16,20},{20,24},{24,28},{28,0},{1,5},{5... | collective-permute-start | bytes 24584 | tf_op jit(solution)/shard_map/ppermute | solution.py:23
  283.7 6.4 %collective-permute-start.92 = (f32[1,8,256]{2,1,0:T(8,128)S(1)}, f32[1,8,256]{2,1,0:T(8,128)S(1)}, u32[]{:S(2)}, u32[]{:S(2)}) collective-permute-start(f32[1,8,256]{2,1,0:T(8,128)S(1)} %get-tuple-element.127), channel_id=1, source_target_pairs={{4,0},{8,4},{12,8},{16,12},{20,16},{24,20},{28,24},{0,28},{5,1},{9... | collective-permute-start | bytes 24584 | tf_op jit(solution)/shard_map/ppermute | solution.py:24
  293.3 6.5 %collective-permute-start.97 = (f32[1,8,256]{2,1,0:T(8,128)S(1)}, f32[1,8,256]{2,1,0:T(8,128)S(1)}, u32[]{:S(2)}, u32[]{:S(2)}) collective-permute-start(f32[1,8,256]{2,1,0:T(8,128)S(1)} %get-tuple-element.124), channel_id=1, source_target_pairs={{0,4},{4,8},{8,12},{12,16},{16,20},{20,24},{24,28},{28,0},{1,5},{5... | collective-permute-start | bytes 24584 | tf_op jit(solution)/shard_map/ppermute | solution.py:23
  293.4 6.4 %collective-permute-start.96 = (f32[1,8,256]{2,1,0:T(8,128)S(1)}, f32[1,8,256]{2,1,0:T(8,128)S(1)}, u32[]{:S(2)}, u32[]{:S(2)}) collective-permute-start(f32[1,8,256]{2,1,0:T(8,128)S(1)} %get-tuple-element.125), channel_id=1, source_target_pairs={{4,0},{8,4},{12,8},{16,12},{20,16},{24,20},{28,24},{0,28},{5,1},{9... | collective-permute-start | bytes 24584 | tf_op jit(solution)/shard_map/ppermute | solution.py:24
  307.7 7.4 %collective-permute-start.100 = (f32[3,16,512]{2,1,0:T(8,128)S(1)}, f32[3,16,512]{2,1,0:T(8,128)S(1)}, u32[]{:S(2)}, u32[]{:S(2)}) collective-permute-start(f32[3,16,512]{2,1,0:T(8,128)S(1)} %get-tuple-element.84), channel_id=1, source_target_pairs={{0,4},{4,8},{8,12},{12,16},{16,20},{20,24},{24,28},{28,0},{1,5},{5... | collective-permute-start | bytes 294920 | tf_op jit(solution)/shard_map/ppermute | solution.py:23
  307.7 7.4 %collective-permute-start.101 = (f32[3,16,512]{2,1,0:T(8,128)S(1)}, f32[3,16,512]{2,1,0:T(8,128)S(1)}, u32[]{:S(2)}, u32[]{:S(2)}) collective-permute-start(f32[3,16,512]{2,1,0:T(8,128)S(1)} %get-tuple-element.85), channel_id=1, source_target_pairs={{4,0},{8,4},{12,8},{16,12},{20,16},{24,20},{28,24},{0,28},{5,1},{9... | collective-permute-start | bytes 294920 | tf_op jit(solution)/shard_map/ppermute | solution.py:24
  315.1 3.9 %collective-permute-start.102 = (f32[10,3,512]{2,1,0:T(4,128)S(1)}, f32[10,3,512]{2,1,0:T(4,128)S(1)}, u32[]{:S(2)}, u32[]{:S(2)}) collective-permute-start(f32[10,3,512]{2,1,0:T(4,128)S(1)} %get-tuple-element.64), channel_id=1, source_target_pairs={{0,1},{1,2},{2,3},{3,0},{4,5},{5,6},{6,7},{7,4},{8,9},{9,10},{10,1... | collective-permute-start | bytes 184328 | tf_op jit(solution)/shard_map/ppermute | solution.py:23
  321.6 6.7 %collective-permute-start.105 = (f32[1,16,512]{2,1,0:T(8,128)S(1)}, f32[1,16,512]{2,1,0:T(8,128)S(1)}, u32[]{:S(2)}, u32[]{:S(2)}) collective-permute-start(f32[1,16,512]{2,1,0:T(8,128)S(1)} %get-tuple-element.82), channel_id=1, source_target_pairs={{0,4},{4,8},{8,12},{12,16},{16,20},{20,24},{24,28},{28,0},{1,5},{5... | collective-permute-start | bytes 98312 | tf_op jit(solution)/shard_map/ppermute | solution.py:23
  321.7 6.7 %collective-permute-start.104 = (f32[1,16,512]{2,1,0:T(8,128)S(1)}, f32[1,16,512]{2,1,0:T(8,128)S(1)}, u32[]{:S(2)}, u32[]{:S(2)}) collective-permute-start(f32[1,16,512]{2,1,0:T(8,128)S(1)} %get-tuple-element.83), channel_id=1, source_target_pairs={{4,0},{8,4},{12,8},{16,12},{20,16},{24,20},{28,24},{0,28},{5,1},{9... | collective-permute-start | bytes 98312 | tf_op jit(solution)/shard_map/ppermute | solution.py:24
  (52 other events, 231.4 us)
where the time goes:
time: 334 us; the launch traced here: 333 us
  starting transfers between devices  156 us (47%)
  waiting for transfers between devices  109 us (33%)
  local copies, waits for them, and re-layouts  42.4 us (13%)
  other arithmetic  24.5 us (7%)
    ppermute x54, starting transfers between devices, padded_2(): after = lax.ppermute(first, axis, down)  143 us
    ppermute x54, waiting for transfers between devices, padded_2(): before = lax.ppermute(last, axis, up)  88.1 us
    reshape x3, local copies, waits for them, and re-layouts, restrict(): return field.reshape(z // 2, 2, y // 2, 2, x // 2, 2).mean(axis=(1, 3, 5))  29.2 us
    ppermute x54, waiting for transfers between devices, padded_2(): after = lax.ppermute(first, axis, down)  20.7 us
    ppermute x54, starting transfers between devices, padded_2(): before = lax.ppermute(last, axis, up)  13 us
    reduce_sum x9, other arithmetic, restrict(): return field.reshape(z // 2, 2, y // 2, 2, x // 2, 2).mean(axis=(1, 3, 5))  12.7 us
  transfers between devices with their start and end apart: 108, of which 72 were waited for; matrix products, arithmetic and copies ran while one was open for 5% of the time, Pallas kernels for 0%

commit v1 on v0

v1 whole, which is shorter than its diff:
```python
import functools

import jax
import jax.numpy as jnp
from jax import lax
from jax.experimental import pallas as pl
from jax.experimental.pallas import tpu as pltpu
from jax.sharding import PartitionSpec as P

DEGREE = 3
COARSE_DEGREE = 4
CYCLES = 2

cheb_low = 0.3
cheb_high = 1.9
heat_step = 4.0
SCALES = (heat_step, heat_step / 4.0, heat_step / 16.0)

HALO = 4
ROWS = 8
MID_REACH = 15
MESH = pl.DeviceIdType.MESH
HIGH = lax.Precision.HIGHEST


def coefficients(steps):
    theta = (cheb_high + cheb_low) / 2.0
    delta = (cheb_high - cheb_low) / 2.0
    sigma = theta / delta
    rho = 1.0 / sigma
    pairs = [(0.0, 1.0 / theta)]
    for _ in range(steps - 1):
        rho_next = 1.0 / (2.0 * sigma - rho)
        pairs.append((rho_next * rho, 2.0 * rho_next / delta))
        rho = rho_next
    return pairs


def window(devices, cells, even):
    reach = -(-MID_REACH // cells)
    count = 2 * reach + 1
    if even:
        count += count % 2
    if count >= devices:
        count = devices
    ahead = count // 2
    return [s if s <= ahead else s - count for s in range(count)]


def select(shape, pick, value):
    rows = lax.broadcasted_iota(jnp.int32, shape, 0)
    columns = lax.broadcasted_iota(jnp.int32, shape, 1)
    return jnp.where(pick(rows, columns), value, 0.0).astype(jnp.float32)


def dot(a, b):
    return jnp.dot(a, b, precision=HIGH, preferred_element_type=jnp.float32)


def narrow(value):
    pairs = select((256, 128), lambda r, c: (r >> 1) == c, 1.0)
    parts = [dot(value[:, i : i + 256], pairs) for i in range(0, value.shape[1], 256)]
    return parts[0] if len(parts) == 1 else jnp.concatenate(parts, axis=1)


def widen(value):
    pairs = select((128, 256), lambda r, c: r == (c >> 1), 1.0)
    parts = [dot(value[:, i : i + 128], pairs) for i in range(0, value.shape[1], 128)]
    return parts[0] if len(parts) == 1 else jnp.concatenate(parts, axis=1)


def beside_of(w, plane):
    planes = w.shape[0]
    here = w[plane]
    rows, columns = here.shape
    lane = lax.broadcasted_iota(jnp.int32, here.shape, 1)
    total = w[lax.rem(plane + 1, planes)] + w[lax.rem(plane + planes - 1, planes)]
    total = total + pltpu.roll(here, 1, 0) + pltpu.roll(here, rows - 1, 0)
    left = jnp.where(lane == 0, 0.0, pltpu.roll(here, 1, 1))
    right = jnp.where(lane == columns - 1, 0.0, pltpu.roll(here, columns - 1, 1))
    return here, total + left + right


def over(planes, own, margin, body):
    if margin is None:
        first, count = 0, planes
    else:
        first, count = planes - margin, own + 2 * margin

    def step(i, carry):
        body(lax.rem(i + first, planes))
        return carry

    lax.fori_loop(0, count, step, 0)


class Level:
    def __init__(self, k, inverse, x, d, w, own, scale):
        self.k, self.inverse, self.x, self.d, self.w = k, inverse, x, d, w
        self.own, self.scale, self.planes = own, scale, k.shape[0]

    def run(self, margin, body):
        over(self.planes, self.own, margin, body)

    def prepare(self, margin):
        def body(p):
            self.inverse[p] = 1.0 / (1.0 + 6.0 * self.scale * self.k[p])

        self.run(margin, body)

    def smooth(self, f, steps, margins, zero):
        now = 0
        for step, (keep, gain) in enumerate(coefficients(steps)):
            old, new = self.w[now], self.w[1 - now]

            def body(p, step=step, keep=keep, gain=gain, old=old, new=new):
                if step == 0 and zero:
                    change = gain * (self.inverse[p] * f[p])
                    field = change
                else:
                    here, beside = beside_of(old, p)
                    field = self.x[p]
                    image = field + self.scale * (6.0 * here - beside)
                    change = gain * (self.inverse[p] * (f[p] - image))
                    if step:
                        change = keep * self.d[p] + change
                    field = field + change
                self.d[p] = change
                self.x[p] = field
                new[p] = self.k[p] * field

            self.run(margins[step], body)
            now = 1 - now
        return self.w[now]

    def residual(self, f, x, w, out, margin):
        def body(p):
            here, beside = beside_of(w, p)
            out[p] = f[p] - (x[p] + self.scale * (6.0 * here - beside))

        self.run(margin, body)


def kernel(sizes, z_window, y_window, source, conduct, adjoint, residual,
           src, k0, inv0, x0, d0, wa0, wb0, r0, r1, early, adj, late,
           k1, inv1, x1, d1, wa1, wb1, t1, f1a, f1b,
           k2, inv2, x2, d2, wa2, wb2, f2, halo_send, halo_recv, mid_send, mid_recv):
    gz, gy = sizes
    own_z, own_y, _ = source.shape
    mz, my = own_z // 2, own_y // 2
    me_z, me_y = lax.axis_index("gz"), lax.axis_index("gy")
    at_z = lambda o: (lax.rem(me_z + o + gz, gz), me_y)
    at_y = lambda o: (me_z, lax.rem(me_y + o + gy, gy))

    barrier = pltpu.get_barrier_semaphore()
    greet_z = sorted({o % gz for o in z_window} | {-o % gz for o in z_window})[1:]
    greet_y = sorted({o % gy for o in y_window} | {-o % gy for o in y_window})[1:]
    for o in greet_z:
        pl.semaphore_signal(barrier, inc=1, device_id=at_z(o), device_id_type=MESH)
    for o in greet_y:
        pl.semaphore_signal(barrier, inc=1, device_id=at_y(o), device_id_type=MESH)
    pl.semaphore_wait(barrier, len(greet_z) + len(greet_y))

    started = []

    def send(from_ref, to_ref, send_sem, recv_sem, device):
        copy = pltpu.make_async_remote_copy(
            src_ref=from_ref, dst_ref=to_ref, send_sem=send_sem, recv_sem=recv_sem,
            device_id=device, device_id_type=MESH)
        copy.start()
        started.append(copy)
        return copy

    zs = 3 * own_z
    ys = own_y + 2 * ROWS

    class Halo:
        def __init__(self, number, own, held, depth):
            self.number, self.held, self.depth, self.count = number, held, depth, 0
            self.z = [
                self.put(own.at[pl.ds(own_z - depth, depth)],
                         held.at[pl.ds(zs - depth, depth), pl.ds(0, own_y)], at_z(1)),
                self.put(own.at[pl.ds(0, depth)],
                         held.at[pl.ds(own_z, depth), pl.ds(0, own_y)], at_z(-1)),
            ]
            self.y = self.rows(own, 0, own_z)

        def put(self, from_ref, to_ref, device):
            i = self.count
            self.count += 1
            return send(from_ref, to_ref, halo_send.at[self.number, i],
                        halo_recv.at[self.number, i], device)

        def rows(self, own, first, count):
            planes = pl.ds(first, count)
            return [
                self.put(own.at[planes, pl.ds(own_y - ROWS, ROWS)],
                         self.held.at[planes, pl.ds(own_y + ROWS, ROWS)], at_y(1)),
                self.put(own.at[planes, pl.ds(0, ROWS)],
                         self.held.at[planes, pl.ds(own_y, ROWS)], at_y(-1)),
            ]

        def forward(self):
            self.z[0].wait_recv()
            self.y += self.rows(self.held, zs - self.depth, self.depth)
            self.z[1].wait_recv()
            self.y += self.rows(self.held, own_z, self.depth)

        def wait(self):
            for copy in self.y:
                copy.wait_recv()

    near = sorted(range(len(z_window)), key=lambda s: abs(z_window[s]))
    wide_y = len(y_window)

    class Gather:
        def __init__(self, number, held):
            self.number, self.held = number, held
            self.z = {}
            for s in near[1:][::-1]:
                self.z[s] = send(
                    self.block(0, 0), self.block(s, 0), mid_send.at[number, s * wide_y],
                    mid_recv.at[number, s * wide_y], at_z(-z_window[s]))
            self.y = []
            self.spread(0)

        def block(self, s, t):
            return self.held.at[pl.ds(s * mz, mz), pl.ds(t * my, my)]

        def spread(self, s):
            for t in range(1, wide_y):
                self.y.append(send(
                    self.block(s, 0), self.block(s, t), mid_send.at[self.number, s * wide_y + t],
                    mid_recv.at[self.number, s * wide_y + t], at_y(-y_window[t])))

        def forward(self):
            for s in near[1:]:
                self.z[s].wait_recv()
                self.spread(s)

        def wait(self):
            for copy in self.y:
                copy.wait_recv()

    def coarsen(fine, coarse, planes, rows):
        lines = select((rows // 2, rows), lambda r, c: r == (c >> 1), 0.125)

        def body(p, carry):
            both = fine[2 * p, pl.ds(0, rows)] + fine[2 * p + 1, pl.ds(0, rows)]
            coarse[p, pl.ds(0, rows // 2)] = narrow(dot(lines, both))
            return carry

        lax.fori_loop(0, planes, body, 0)

    fine = Level(k0, inv0, x0, d0, (wa0, wb0), own_z, SCALES[0])
    middle = Level(k1, inv1, x1, d1, (wa1, wb1), None, SCALES[1])
    low = Level(k2, inv2, x2, d2, (wa2, wb2), None, SCALES[2])
    mid_planes, mid_rows, low_planes = k1.shape[0], k1.shape[1], k2.shape[0]

    source_halo = Halo(0, source, src, HALO - 1)
    conduct_halo = Halo(1, conduct, k0, HALO)
    src[pl.ds(0, own_z), pl.ds(0, own_y)] = source[...]
    k0[pl.ds(0, own_z), pl.ds(0, own_y)] = conduct[...]
    coarsen(k0, k1, mz, own_y)
    conduct_mid = Gather(0, k1)
    source_halo.forward()
    conduct_halo.forward()
    conduct_mid.forward()
    source_halo.wait()
    conduct_halo.wait()
    fine.prepare(HALO)

    def down(f, f1, number, held, halo_number, depth):
        w = fine.smooth(f, DEGREE, (3, 2, 1), True)
        held[pl.ds(0, own_z), pl.ds(0, own_y)] = x0[pl.ds(0, own_z), pl.ds(0, own_y)]
        fine.residual(f, x0, w, r0, 0)
        coarsen(r0, f1, mz, own_y)
        gather = Gather(number, f1)
        halo = Halo(halo_number, held.at[pl.ds(0, own_z), pl.ds(0, own_y)], held, depth)
        gather.forward()
        halo.forward()
        return gather, halo

    def solve(f1):
        w = middle.smooth(f1, DEGREE, (None,) * DEGREE, True)
        middle.residual(f1, x1, w, t1, None)
        coarsen(t1, f2, low_planes, mid_rows)
        low.smooth(f2, COARSE_DEGREE, (None,) * COARSE_DEGREE, True)
        lines = select((mid_rows, mid_rows // 2), lambda r, c: (r >> 1) == c, 1.0)

        def body(p, carry):
            add = widen(dot(lines, x2[p]))
            for half in range(2):
                field = x1[2 * p + half] + add
                x1[2 * p + half] = field
                wa1[2 * p + half] = k1[2 * p + half] * field
            return carry

        lax.fori_loop(0, low_planes, body, 0)
        middle.smooth(f1, DEGREE, (None,) * DEGREE, False)

    def up(f, held, margin):
        def pick(r, c):
            own = (r < own_y + ROWS) & ((r >> 1) == c)
            return own | ((r >= own_y + ROWS) & ((r >> 1) - (ys >> 1) + mid_rows == c))

        lines = select((ys, mid_rows), pick, 1.0)
        pairs = zs // 2
        sides = (margin + 1) // 2

        def body(i, carry):
            pair = lax.rem(i + pairs - sides, pairs)
            late_pair = (pair >= own_z).astype(jnp.int32)
            add = widen(dot(lines, x1[pair + late_pair * (mid_planes - pairs)]))
            for half in range(2):
                p = 2 * pair + half
                field = held[p] + add
                x0[p] = field
                wa0[p] = k0[p] * field
            return carry

        lax.fori_loop(0, mz + 2 * sides, body, 0)
        return fine.smooth(f, DEGREE, (margin - 1, margin - 2, margin - 3), False)

    gather, halo = down(src, f1a, 1, early, 2, HALO - 1)
    conduct_mid.wait()
    middle.prepare(None)
    coarsen(k1, k2, low_planes, mid_rows)
    low.prepare(None)
    gather.wait()
    solve(f1a)
    halo.wait()
    up(src, early, HALO - 1)
    adj[pl.ds(0, own_z), pl.ds(0, own_y)] = x0[pl.ds(0, own_z), pl.ds(0, own_y)]
    halo = Halo(3, adj.at[pl.ds(0, own_z), pl.ds(0, own_y)], adj, HALO)
    halo.forward()
    halo.wait()

    def weigh(p):
        wa0[p] = k0[p] * adj[p]

    fine.run(HALO, weigh)
    fine.residual(src, adj, wa0, r1, HALO - 1)

    gather, halo = down(r1, f1b, 2, late, 4, HALO)
    gather.wait()
    solve(f1b)
    halo.wait()
    up(r1, late, HALO)

    def finish(p):
        field = adj[p] + x0[p]
        x0[p] = field
        wa0[p] = k0[p] * field

    fine.run(1, finish)
    fine.residual(src, x0, wa0, r0, 0)
    adjoint[...] = x0[pl.ds(0, own_z), pl.ds(0, own_y)]
    residual[...] = r0[pl.ds(0, own_z), pl.ds(0, own_y)]
    for copy in started:
        copy.wait_send()


def local(sizes, source, conduct):
    own_z, own_y, nx = source.shape
    z_window = window(sizes[0], own_z // 2, False)
    y_window = window(sizes[1], own_y // 2, True)
    fine = (3 * own_z, own_y + 2 * ROWS, nx)
    mid = (len(z_window) * own_z // 2, len(y_window) * own_y // 2, nx // 2)
    low = tuple(n // 2 for n in mid)
    slots = len(z_window) * len(y_window)
    vmem = lambda shape, count: [pltpu.VMEM(shape, jnp.float32)] * count
    whole = pl.BlockSpec(memory_space=pltpu.VMEM)
    return pl.pallas_call(
        functools.partial(kernel, sizes, z_window, y_window),
        out_shape=[jax.ShapeDtypeStruct(source.shape, jnp.float32)] * 2,
        in_specs=[whole] * 2,
        out_specs=[whole] * 2,
        scratch_shapes=vmem(fine, 12) + vmem(mid, 9) + vmem(low, 7) + [
            pltpu.SemaphoreType.DMA((5, 8)),
            pltpu.SemaphoreType.DMA((5, 8)),
            pltpu.SemaphoreType.DMA((3, slots)),
            pltpu.SemaphoreType.DMA((3, slots)),
        ],
        compiler_params=pltpu.CompilerParams(
            collective_id=0, has_side_effects=True, vmem_limit_bytes=56 * 1024 * 1024
        ),
    )(source, conduct)


def solution(mesh):
    spec = P("gz", "gy", None)
    sizes = (mesh.shape["gz"], mesh.shape["gy"])
    return jax.shard_map(
        functools.partial(local, sizes),
        mesh=mesh,
        in_specs=(spec, spec),
        out_specs=(spec, spec),
        check_vma=False,
    )
```

time: 334 us -> 118 us (0.35)
  starting transfers between devices: 156 us -> 0 us
  Pallas kernels: 0 us -> 114 us
  waiting for transfers between devices: 109 us -> 0 us
  local copies, waits for them, and re-layouts: 42.4 us -> 2.26 us
  other arithmetic: 24.5 us -> 0 us
    ppermute x108 -> x0, starting transfers between devices: 156 us -> none  [the longest x54 143 us: padded_2(): after = lax.ppermute(first, axis, down)]
    pallas_call x0 -> x1, Pallas kernels: none -> 114 us  [local(): pl.pallas_call(functools.partial(kernel, sizes, z_window, y_window), out_...]
    ppermute x108 -> x0, waiting for transfers between devices: 109 us -> none  [the longest x54 88.1 us: padded_2(): before = lax.ppermute(last, axis, up)]
    reshape x9 -> x0, local copies, waits for them, and re-layouts: 33.3 us -> none  [the longest x3 29.2 us: restrict(): return field.reshape(z // 2, 2, y // 2, 2, x // 2, 2).mean(axis=(1, 3, 5))]
    reduce_sum x9 -> x0, other arithmetic: 12.7 us -> none  [restrict(): return field.reshape(z // 2, 2, y // 2, 2, x // 2, 2).mean(axis=(1, 3, 5))]
    mul x32 -> x0, other arithmetic: 7.83 us -> none  [the longest x11 6.07 us: margin_apply(): w = conduct * field]
  transfers between devices with their start and end apart: 108 -> 0, of which waited for: 72 -> 0; matrix products, arithmetic and copies ran while one was open for 5% -> 0% of each run, Pallas kernels for 0% -> 0%
where the time goes in v1:
time: 118 us; the launch traced here: 117 us
  Pallas kernels  114 us (97%)
  local copies, waits for them, and re-layouts  2.26 us (2%)
    pallas_call x1, Pallas kernels, local(): pl.pallas_call(functools.partial(kernel, sizes, z_window, y_window), out_...  114 us

profile of v1, /device:TPU:0, one launch (start us, length us, event | category | flops | bytes accessed | tf_op | source)
XLA Modules:
  0.0 117.4 jit_solution(9968589745467476509)
XLA Ops:
  0.6 114.5 %shard_map.41 = (f32[4,16,512]{2,1,0:T(8,128)}, f32[4,16,512]{2,1,0:T(8,128)}) custom-call(f32[4,16,512]{2,1,0:T(8,128)} %source.1, f32[4,16,512]{2,1,0:T(8,128)} %conduct.1), custom_call_target="tpu_custom_call" | custom-call | tf_op jit(solution)/shard_map/pallas_call | solution.py:374
  115.1 0.0 copy-start
  115.1 1.6 %copy.6 = f32[4,16,512]{2,1,0:T(8,128)} copy(f32[4,16,512]{2,1,0:T(8,128)} %get-tuple-element.4) | data formatting | bytes 262144
  116.8 0.0 copy-done
  116.8 0.7 copy.7
Async XLA Ops:
  115.1 1.6 %copy-start = (f32[4,16,512]{2,1,0:T(8,128)S(1)}, f32[4,16,512]{2,1,0:T(8,128)}, u32[]{:S(2)}) copy-start(f32[4,16,512]{2,1,0:T(8,128)} %get-tuple-element.5) | copy-start | bytes 393220

commit v2 on v1

--- a/solution.py
+++ b/solution.py
@@ -20,7 +20,7 @@
 ROWS = 8
 MID_REACH = 15
 MESH = pl.DeviceIdType.MESH
-HIGH = lax.Precision.HIGHEST
+LANES = 128
 
 
 def coefficients(steps):
@@ -50,35 +50,68 @@
 def select(shape, pick, value):
     rows = lax.broadcasted_iota(jnp.int32, shape, 0)
     columns = lax.broadcasted_iota(jnp.int32, shape, 1)
-    return jnp.where(pick(rows, columns), value, 0.0).astype(jnp.float32)
+    return jnp.where(pick(rows, columns), value, 0.0).astype(jnp.bfloat16)
+
+
+def parts_of(value):
+    parts = []
+    for _ in range(3):
+        parts.append(value.astype(jnp.bfloat16))
+        value = value - parts[-1].astype(jnp.float32)
+    return parts
 
 
 def dot(a, b):
-    return jnp.dot(a, b, precision=HIGH, preferred_element_type=jnp.float32)
+    return jnp.dot(a, b, preferred_element_type=jnp.float32)
+
+
+def pick_rows(lines, value):
+    high, middle, low = (dot(lines, part) for part in parts_of(value))
+    return high + (middle + low)
+
+
+def pick_columns(value, columns):
+    high, middle, low = (dot(part, columns) for part in parts_of(value))
+    return high + (middle + low)
+
+
+def chunks(value):
+    return [value[:, i : i + LANES] for i in range(0, value.shape[1], LANES)]
+
+
+def join(parts):
+    return parts[0] if len(parts) == 1 else jnp.concatenate(parts, axis=1)
 
 
 def narrow(value):
-    pairs = select((256, 128), lambda r, c: (r >> 1) == c, 1.0)
-    parts = [dot(value[:, i : i + 256], pairs) for i in range(0, value.shape[1], 256)]
-    return parts[0] if len(parts) == 1 else jnp.concatenate(parts, axis=1)
+    parts = chunks(value)
+    return join([parts[i] + parts[i + 1] for i in range(0, len(parts), 2)])
 
 
 def widen(value):
-    pairs = select((128, 256), lambda r, c: r == (c >> 1), 1.0)
-    parts = [dot(value[:, i : i + 128], pairs) for i in range(0, value.shape[1], 128)]
-    return parts[0] if len(parts) == 1 else jnp.concatenate(parts, axis=1)
+    return join([part for part in chunks(value) for _ in range(2)])
+
+
+def along_x(here):
+    parts = chunks(here)
+    lane = lax.broadcasted_iota(jnp.int32, parts[0].shape, 1)
+    first = jnp.where(lane == 0, 0.0, pltpu.roll(parts[-1], 1, 1))
+    last = jnp.where(lane == LANES - 1, 0.0, pltpu.roll(parts[0], LANES - 1, 1))
+    around = [first] + parts + [last]
+    return join([around[j] + around[j + 2] for j in range(len(parts))])
 
 
 def beside_of(w, plane):
     planes = w.shape[0]
     here = w[plane]
-    rows, columns = here.shape
-    lane = lax.broadcasted_iota(jnp.int32, here.shape, 1)
+    rows = here.shape[0]
     total = w[lax.rem(plane + 1, planes)] + w[lax.rem(plane + planes - 1, planes)]
     total = total + pltpu.roll(here, 1, 0) + pltpu.roll(here, rows - 1, 0)
-    left = jnp.where(lane == 0, 0.0, pltpu.roll(here, 1, 1))
-    right = jnp.where(lane == columns - 1, 0.0, pltpu.roll(here, columns - 1, 1))
-    return here, total + left + right
+    return here, total + along_x(here)
+
+
+def unrolled(count):
+    return 4 if count % 4 == 0 else 2 if count % 2 == 0 else 1
 
 
 def over(planes, own, margin, body):
@@ -91,7 +124,7 @@
         body(lax.rem(i + first, planes))
         return carry
 
-    lax.fori_loop(0, count, step, 0)
+    lax.fori_loop(0, count, step, 0, unroll=unrolled(count))
 
 
 class Level:
@@ -247,28 +280,42 @@
 
         def body(p, carry):
             both = fine[2 * p, pl.ds(0, rows)] + fine[2 * p + 1, pl.ds(0, rows)]
-            coarse[p, pl.ds(0, rows // 2)] = narrow(dot(lines, both))
+            coarse[p, pl.ds(0, rows // 2)] = pick_rows(lines, narrow(both))
             return carry
 
-        lax.fori_loop(0, planes, body, 0)
+        lax.fori_loop(0, planes, body, 0, unroll=unrolled(planes))
 
     fine = Level(k0, inv0, x0, d0, (wa0, wb0), own_z, SCALES[0])
     middle = Level(k1, inv1, x1, d1, (wa1, wb1), None, SCALES[1])
     low = Level(k2, inv2, x2, d2, (wa2, wb2), None, SCALES[2])
     mid_planes, mid_rows, low_planes = k1.shape[0], k1.shape[1], k2.shape[0]
 
-    source_halo = Halo(0, source, src, HALO - 1)
-    conduct_halo = Halo(1, conduct, k0, HALO)
-    src[pl.ds(0, own_z), pl.ds(0, own_y)] = source[...]
-    k0[pl.ds(0, own_z), pl.ds(0, own_y)] = conduct[...]
+    nx = source.shape[2]
+    share = nx // LANES
+
+    def deal(r, c):
+        return r == share * (c & (LANES - 1)) + c // LANES
+
+    def own_of(ref):
+        return ref.at[pl.ds(0, own_z), pl.ds(0, own_y)]
+
+    def permuted(value, pick):
+        columns = select((nx, nx), pick, 1.0)
+        flat = value.reshape(own_z * own_y, nx)
+        return pick_columns(flat, columns).reshape(own_z, own_y, nx)
+
+    own_of(k0)[...] = permuted(conduct[...], deal)
+    conduct_halo = Halo(1, own_of(k0), k0, HALO)
+    own_of(src)[...] = permuted(source[...], deal)
+    source_halo = Halo(0, own_of(src), src, HALO - 1)
     coarsen(k0, k1, mz, own_y)
     conduct_mid = Gather(0, k1)
+    conduct_halo.forward()
     source_halo.forward()
-    conduct_halo.forward()
+    conduct_halo.wait()
+    source_halo.wait()
+    fine.prepare(HALO)
     conduct_mid.forward()
-    source_halo.wait()
-    conduct_halo.wait()
-    fine.prepare(HALO)
 
     def down(f, f1, number, held, halo_number, depth):
         w = fine.smooth(f, DEGREE, (3, 2, 1), True)
@@ -278,25 +325,25 @@
         gather = Gather(number, f1)
         halo = Halo(halo_number, held.at[pl.ds(0, own_z), pl.ds(0, own_y)], held, depth)
         gather.forward()
+        return gather, halo
+
+    def solve(f1, halo):
+        w = middle.smooth(f1, DEGREE, (None,) * DEGREE, True)
         halo.forward()
-        return gather, halo
-
-    def solve(f1):
-        w = middle.smooth(f1, DEGREE, (None,) * DEGREE, True)
         middle.residual(f1, x1, w, t1, None)
         coarsen(t1, f2, low_planes, mid_rows)
         low.smooth(f2, COARSE_DEGREE, (None,) * COARSE_DEGREE, True)
         lines = select((mid_rows, mid_rows // 2), lambda r, c: (r >> 1) == c, 1.0)
 
         def body(p, carry):
-            add = widen(dot(lines, x2[p]))
+            add = widen(pick_rows(lines, x2[p]))
             for half in range(2):
                 field = x1[2 * p + half] + add
                 x1[2 * p + half] = field
                 wa1[2 * p + half] = k1[2 * p + half] * field
             return carry
 
-        lax.fori_loop(0, low_planes, body, 0)
+        lax.fori_loop(0, low_planes, body, 0, unroll=unrolled(low_planes))
         middle.smooth(f1, DEGREE, (None,) * DEGREE, False)
 
     def up(f, held, margin):
@@ -311,7 +358,7 @@
         def body(i, carry):
             pair = lax.rem(i + pairs - sides, pairs)
             late_pair = (pair >= own_z).astype(jnp.int32)
-            add = widen(dot(lines, x1[pair + late_pair * (mid_planes - pairs)]))
+            add = widen(pick_rows(lines, x1[pair + late_pair * (mid_planes - pairs)]))
             for half in range(2):
                 p = 2 * pair + half
                 field = held[p] + add
@@ -319,7 +366,7 @@
                 wa0[p] = k0[p] * field
             return carry
 
-        lax.fori_loop(0, mz + 2 * sides, body, 0)
+        lax.fori_loop(0, mz + 2 * sides, body, 0, unroll=unrolled(mz + 2 * sides))
         return fine.smooth(f, DEGREE, (margin - 1, margin - 2, margin - 3), False)
 
     gather, halo = down(src, f1a, 1, early, 2, HALO - 1)
@@ -328,7 +375,7 @@
     coarsen(k1, k2, low_planes, mid_rows)
     low.prepare(None)
     gather.wait()
-    solve(f1a)
+    solve(f1a, halo)
     halo.wait()
     up(src, early, HALO - 1)
     adj[pl.ds(0, own_z), pl.ds(0, own_y)] = x0[pl.ds(0, own_z), pl.ds(0, own_y)]
@@ -344,7 +391,7 @@
 
     gather, halo = down(r1, f1b, 2, late, 4, HALO)
     gather.wait()
-    solve(f1b)
+    solve(f1b, halo)
     halo.wait()
     up(r1, late, HALO)
 
@@ -355,8 +402,8 @@
 
     fine.run(1, finish)
     fine.residual(src, x0, wa0, r0, 0)
-    adjoint[...] = x0[pl.ds(0, own_z), pl.ds(0, own_y)]
-    residual[...] = r0[pl.ds(0, own_z), pl.ds(0, own_y)]
+    for ref, out in ((x0, adjoint), (r0, residual)):
+        out[...] = permuted(own_of(ref)[...], lambda r, c: deal(c, r))
     for copy in started:
         copy.wait_send()
 

time: 118 us -> 82.1 us (0.70)
  Pallas kernels: 114 us -> 78.8 us
    pallas_call x1, Pallas kernels: 114 us -> 78.8 us  [local(): pl.pallas_call(functools.partial(kernel, sizes, z_window, y_window), out_...]
where the time goes in v2:
time: 82.1 us; the launch traced here: 81.7 us
  Pallas kernels  78.8 us (96%)
  local copies, waits for them, and re-layouts  2.26 us (3%)
    pallas_call x1, Pallas kernels, local(): pl.pallas_call(functools.partial(kernel, sizes, z_window, y_window), out_...  78.8 us
    unnamed x4, local copies, waits for them, and re-layouts  2.26 us

profile of v2, /device:TPU:0, one launch (start us, length us, event | category | flops | bytes accessed | tf_op | source)
XLA Modules:
  0.0 81.7 jit_solution(1211853198076265573)
XLA Ops:
  0.6 78.8 %shard_map.41 = (f32[4,16,512]{2,1,0:T(8,128)}, f32[4,16,512]{2,1,0:T(8,128)}) custom-call(f32[4,16,512]{2,1,0:T(8,128)} %source.1, f32[4,16,512]{2,1,0:T(8,128)} %conduct.1), custom_call_target="tpu_custom_call" | custom-call | tf_op jit(solution)/shard_map/pallas_call | solution.py:421
  79.4 0.0 copy-start
  79.4 1.6 %copy.6 = f32[4,16,512]{2,1,0:T(8,128)} copy(f32[4,16,512]{2,1,0:T(8,128)} %get-tuple-element.4) | data formatting | bytes 262144
  81.0 0.0 copy-done
  81.0 0.7 copy.7
Async XLA Ops:
  79.4 1.6 %copy-start = (f32[4,16,512]{2,1,0:T(8,128)S(1)}, f32[4,16,512]{2,1,0:T(8,128)}, u32[]{:S(2)}) copy-start(f32[4,16,512]{2,1,0:T(8,128)} %get-tuple-element.5) | copy-start | bytes 393220
